TPU v7x, 32 devices: a whole 2x2x4 slice. The times are simulated.
32 devices in a mesh: seq: 8 (over z, y), head: 4 (over x, core).
Axes of the slice: x: 2, y: 2, z: 4, core: 2. Of those that a mesh axis runs over, the one named last changes fastest.
Arguments:
- queries: bfloat16 [1024, 1536], P('seq', 'head'), may hold values from -400 to 400
- latent: bfloat16 [1024, 320], P(('seq', 'head')), may hold values from -6 to 6
- w_kv_up: bfloat16 [256, 2048], P(None, 'head'), may hold values from -0.375 to 0.375
Outputs:
- attended: bfloat16 [1024, 1024], P('seq', 'head')
All inputs are finite; a program needn't handle non-finite values.
Results may differ from a plain program's by a relative error of at most 0.004.
Values may be sent and summed in bfloat16 or wider, within the bound.
A program may use at most 64 MiB of HBM per device.

v0:
```python
import math

import jax
import jax.numpy as jnp
from jax import lax
from jax.sharding import PartitionSpec as P

D_LATENT = 256
ROPE = 64
NOPE = 128
VDIM = 128


MASKED = -1e30


def from_behind(shard, axis, by):
    length = lax.axis_size(axis)
    pairs = [(i, i + by) for i in range(length) if 0 <= i + by < length]
    return lax.ppermute(shard, axis, pairs)


def attend(state, key_block, key_start, setup):
    query_side, query_rope, query_pos, w_kv_up, absorb = setup
    numerator, running_max, totals = state
    local_heads = query_rope.shape[1]
    key_count = key_block.shape[0]
    highest = lax.Precision.HIGHEST
    key_latent = key_block[:, :D_LATENT]
    key_rope = key_block[:, D_LATENT:]
    key_value = jnp.dot(key_latent, w_kv_up, preferred_element_type=jnp.float32)
    key_value = key_value.reshape(key_count, local_heads, NOPE + VDIM)
    scores = jnp.einsum("qhd,khd->hqk", query_side, key_value[:, :, :NOPE], precision=highest)
    scores = scores + jnp.einsum(
        "qhd,kd->hqk", query_rope, key_rope, preferred_element_type=jnp.float32
    )
    scores = scores * (NOPE + ROPE) ** (-0.5)
    key_pos = key_start + lax.iota(jnp.int32, key_count)
    allowed = (key_pos[None, :] <= query_pos[:, None]) & (key_pos[None, :] >= 0)
    scores = jnp.where(allowed[None], scores, MASKED)
    new_max = jnp.maximum(running_max, jnp.max(scores, axis=2))
    factor = jnp.exp(running_max - new_max)
    weights = jnp.where(allowed[None], jnp.exp(scores - new_max[:, :, None]), 0.0)
    totals = totals * factor + jnp.sum(weights, axis=2)
    rounded = weights.astype(jnp.bfloat16)
    update = jnp.einsum(
        "hqk,khd->hqd", rounded.astype(jnp.float32), key_value[:, :, NOPE:], precision=highest
    )
    numerator = numerator * factor[:, :, None] + update
    return (numerator, new_max, totals)


def attend_blocks(state, keys, key_start, setup):
    key_total = keys.shape[0]
    block_rows = key_total if key_total <= 1024 else math.gcd(key_total, 1024)
    block_count = key_total // block_rows

    def one_block(block_index, inner):
        offset = block_index * block_rows
        piece = lax.dynamic_slice_in_dim(keys, offset, block_rows, 0)
        return attend(inner, piece, key_start + offset, setup)

    if block_count == 1:
        return one_block(0, state)
    return lax.fori_loop(0, block_count, one_block, state)


def prepare(query_rows, query_pos, w_kv_up):
    row_count = query_rows.shape[0]
    local_heads = w_kv_up.shape[1] // (NOPE + VDIM)
    query_all = query_rows.reshape(row_count, local_heads, NOPE + ROPE)
    query_side = query_all[:, :, :NOPE].astype(jnp.float32)
    width = VDIM
    setup = (query_side, query_all[:, :, NOPE:], query_pos, w_kv_up, False)
    start_state = (
        jnp.zeros((local_heads, row_count, width), jnp.float32),
        jnp.full((local_heads, row_count), MASKED, jnp.float32),
        jnp.zeros((local_heads, row_count), jnp.float32),
    )
    return (setup, start_state)


def finish(state, w_kv_up):
    numerator, running_max, totals = state
    local_heads = w_kv_up.shape[1] // (NOPE + VDIM)
    row_count = totals.shape[1]
    result = numerator / totals[:, :, None]
    return (
        jnp.transpose(result, (1, 0, 2)).reshape(row_count, local_heads * VDIM).astype(jnp.bfloat16)
    )


def body(queries, latent, w_kv_up):
    group_rows = queries.shape[0]
    seq_groups = lax.axis_size("seq")
    group_index = lax.axis_index("seq")
    query_pos = group_index * group_rows + lax.iota(jnp.int32, group_rows)
    setup, state = prepare(queries, query_pos, w_kv_up)
    gathered = lax.all_gather(latent, "head", axis=0, tiled=True)
    state = attend(state, gathered, group_index * group_rows, setup)
    history = gathered
    span_groups = 1
    while span_groups < seq_groups:
        arrived = from_behind(history, "seq", span_groups)
        state = attend_blocks(
            state, arrived, (group_index - 2 * span_groups + 1) * group_rows, setup
        )
        if 2 * span_groups < seq_groups:
            history = jnp.concatenate([arrived, history], axis=0)
        span_groups = span_groups * 2
    return finish(state, w_kv_up)


def solution(mesh):
    in_specs = (P("seq", "head"), P(("seq", "head"), None), P(None, "head"))
    out_specs = P("seq", "head")
    return jax.shard_map(body, mesh=mesh, in_specs=in_specs, out_specs=out_specs, check_vma=False)
```

profile of v0, /device:TPU:25, one launch (start us, length us, event | category | flops | bytes accessed | tf_op | source)
XLA Modules:
  0.0 42.7 jit_solution(3402798072797051808)
XLA Ops:
  0.0 6.2 %all_gather.3 = bf16[128,320]{1,0:T(8,128)(2,1)S(1)} all-gather(bf16[32,320]{1,0:T(8,128)(2,1)} %param.4), channel_id=1, replica_groups=mesh['seq'=8,'head'=4] {'head'}, dimensions={0}, use_global_device_ids=true | all-gather | bytes 102400 | tf_op jit(solution)/shard_map/all_gather | solution.py:99
  6.3 3.1 %collective-permute-start = (bf16[128,320]{0,1:T(8,128)(2,1)S(1)}, bf16[128,320]{0,1:T(8,128)(2,1)S(1)}, u32[]{:S(2)}, u32[]{:S(2)}) collective-permute-start(bf16[128,320]{0,1:T(8,128)(2,1)S(1)} %copy.39), channel_id=1, source_target_pairs={{0,4},{4,8},{8,12},{12,16},{16,20},{20,24},{24,28},{1,5},{5,9},{9,... | collective-permute-start | bytes 245768 | tf_op jit(solution)/shard_map/ppermute | solution.py:20
  10.4 0.2 compare_and_fusion
  10.7 0.2 fusion.90
  11.1 1.8 %collective-permute-done = bf16[128,320]{0,1:T(8,128)(2,1)S(1)} collective-permute-done((bf16[128,320]{0,1:T(8,128)(2,1)S(1)}, bf16[128,320]{0,1:T(8,128)(2,1)S(1)}, u32[]{:S(2)}, u32[]{:S(2)}) %collective-permute-start) | collective-permute-done | bytes 81952 | tf_op jit(solution)/shard_map/ppermute | solution.py:20
  12.9 1.3 %collective-permute-start.1 = (bf16[256,320]{0,1:T(8,128)(2,1)S(1)}, bf16[256,320]{0,1:T(8,128)(2,1)S(1)}, u32[]{:S(2)}, u32[]{:S(2)}) collective-permute-start(bf16[256,320]{0,1:T(8,128)(2,1)S(1)} %pad_maximum_fusion.1), channel_id=1, source_target_pairs={{0,8},{4,12},{8,16},{12,20},{16,24},{20,28},{1,9},{5,13},{9,17},{1... | collective-permute-start | bytes 491528 | tf_op jit(solution)/shard_map/ppermute | solution.py:20
  14.2 0.2 fusion.51
  14.7 0.2 convolution_bitcast_fusion.7
  14.9 0.2 fusion.89
  15.2 4.4 %collective-permute-done.1 = bf16[256,320]{0,1:T(8,128)(2,1)S(1)} collective-permute-done((bf16[256,320]{0,1:T(8,128)(2,1)S(1)}, bf16[256,320]{0,1:T(8,128)(2,1)S(1)}, u32[]{:S(2)}, u32[]{:S(2)}) %collective-permute-start.1) | collective-permute-done | bytes 163872 | tf_op jit(solution)/shard_map/ppermute | solution.py:20
  19.6 1.3 %collective-permute-start.2 = (bf16[512,320]{0,1:T(8,128)(2,1)S(1)}, bf16[512,320]{0,1:T(8,128)(2,1)S(1)}, u32[]{:S(2)}, u32[]{:S(2)}) collective-permute-start(bf16[512,320]{0,1:T(8,128)(2,1)S(1)} %pad_maximum_fusion), channel_id=1, source_target_pairs={{0,16},{4,20},{8,24},{12,28},{1,17},{5,21},{9,25},{13,29},{2,18},{... | collective-permute-start | bytes 983048 | tf_op jit(solution)/shard_map/ppermute | solution.py:20
  20.9 0.2 fusion.36
  21.2 0.3 reshape.300
  21.7 0.2 convolution_bitcast_fusion.2
  21.9 0.2 fusion.88
  22.2 16.7 %collective-permute-done.2 = bf16[512,320]{0,1:T(8,128)(2,1)S(1)} collective-permute-done((bf16[512,320]{0,1:T(8,128)(2,1)S(1)}, bf16[512,320]{0,1:T(8,128)(2,1)S(1)}, u32[]{:S(2)}, u32[]{:S(2)}) %collective-permute-start.2) | collective-permute-done | bytes 327712 | tf_op jit(solution)/shard_map/ppermute | solution.py:20
  38.9 0.3 fusion.26
  39.3 0.6 %convolution_bitcast_fusion.1 = f32[2,128,512]{1,2,0:T(8,128)S(1)} fusion(f32[512,2,256]{0,2,1:T(8,128)S(1)} %bitcast.164, bf16[128,2,192]{0,2,1:T(8,128)(2,1)S(1)} %bitcast.162), kind=kOutput, calls=%fused_computation.2 | convolution fusion | flops 201326592 | bytes 1114112 | tf_op jit(solution)/shard_map/qhd,khd->hqk/dot_general | solution.py:33
  39.9 0.3 fusion.87
  40.5 0.3 fusion.15
  40.8 0.3 fusion.16
  41.1 0.4 %fusion.9 = f32[128,2,128]{0,2,1:T(8,128)S(1)} fusion(f32[128,2,128]{0,2,1:T(8,128)S(1)} %fusion.16, f32[256,2,128]{2,1,0:T(2,128)S(1)} %get-tuple-element.11, f32[2,128,256]{1,2,0:T(8,128)S(1)} %get-tuple-element.25, f32[2,128]{1,0:T(2,128)S(1)} %get-tuple-element.9, pred[128,256]{0,1:T(8,128)(4,1)S(1)} %compare_and_fusion.1, ...), kind=kOutput, calls=%fused_computation.15 | convolution fusion | flops 100925440 | bytes 821248 | tf_op jit(solution)/shard_map/hqk,khd->hqd/dot_general | solution.py:46
  41.5 0.4 %fusion.20 = bf16[128,2,128]{0,2,1:T(8,128)(2,1)S(1)} fusion(f32[128,2,128]{0,2,1:T(8,128)S(1)} %fusion.9, f32[512,2,256]{0,2,1:T(8,128)S(1)} %bitcast.165, f32[2,128,512]{1,2,0:T(8,128)S(1)} %get-tuple-element.23, f32[2,128]{1,0:T(2,128)S(1)} %get-tuple-element.8, pred[128,512]{0,1:T(8,128)(4,1)S(1)} %compare_and_fusion, f32[128,2]{0,1:T(2,128)S(1)} %get-tuple-element.5), kind=kOutput, calls=%fused_computation.32 | convolution fusion | flops 201818112 | bytes 1312768 | tf_op jit(solution)/shard_map/hqk,khd->hqd/dot_general | solution.py:46
  42.0 0.7 %copy.53 = bf16[128,256]{1,0:T(8,128)(2,1)} copy(bf16[128,256]{0,1:T(8,128)(2,1)S(1)} %bitcast.166) | data formatting | bytes 131072 | tf_op jit(solution)/shard_map/convert_element_type | solution.py:89
  (30 shorter events, 2.0 us)
Async XLA Ops:
  0.0 9.9 %copy-start = (bf16[256,512]{1,0:T(8,128)(2,1)S(1)}, bf16[256,512]{1,0:T(8,128)(2,1)}, u32[]{:S(2)}) copy-start(bf16[256,512]{1,0:T(8,128)(2,1)} %param.5) | copy-start | bytes 786436
  6.2 3.4 %copy-start.1 = (bf16[128,384]{1,0:T(8,128)(2,1)S(1)}, bf16[128,384]{1,0:T(8,128)(2,1)}, u32[]{:S(2)}) copy-start(bf16[128,384]{1,0:T(8,128)(2,1)} %param.3) | copy-start | bytes 294916
  6.3 6.6 %collective-permute-start = (bf16[128,320]{0,1:T(8,128)(2,1)S(1)}, bf16[128,320]{0,1:T(8,128)(2,1)S(1)}, u32[]{:S(2)}, u32[]{:S(2)}) collective-permute-start(bf16[128,320]{0,1:T(8,128)(2,1)S(1)} %copy.39), channel_id=1, source_target_pairs={{0,4},{4,8},{8,12},{12,16},{16,20},{20,24},{24,28},{1,5},{5,9},{9,... | collective-permute-start | bytes 245768 | tf_op jit(solution)/shard_map/ppermute | solution.py:20
  12.9 6.6 %collective-permute-start.1 = (bf16[256,320]{0,1:T(8,128)(2,1)S(1)}, bf16[256,320]{0,1:T(8,128)(2,1)S(1)}, u32[]{:S(2)}, u32[]{:S(2)}) collective-permute-start(bf16[256,320]{0,1:T(8,128)(2,1)S(1)} %pad_maximum_fusion.1), channel_id=1, source_target_pairs={{0,8},{4,12},{8,16},{12,20},{16,24},{20,28},{1,9},{5,13},{9,17},{1... | collective-permute-start | bytes 491528 | tf_op jit(solution)/shard_map/ppermute | solution.py:20
  19.6 19.3 %collective-permute-start.2 = (bf16[512,320]{0,1:T(8,128)(2,1)S(1)}, bf16[512,320]{0,1:T(8,128)(2,1)S(1)}, u32[]{:S(2)}, u32[]{:S(2)}) collective-permute-start(bf16[512,320]{0,1:T(8,128)(2,1)S(1)} %pad_maximum_fusion), channel_id=1, source_target_pairs={{0,16},{4,20},{8,24},{12,28},{1,17},{5,21},{9,25},{13,29},{2,18},{... | collective-permute-start | bytes 983048 | tf_op jit(solution)/shard_map/ppermute | solution.py:20
where the time goes:
time: 42.9 us; the launch traced here: 42.7 us
  waiting for transfers between devices  23 us (54%)
  blocking collectives  6.16 us (14%)
  starting transfers between devices  5.73 us (13%)
  matrix products  4.62 us (11%)
  local copies, waits for them, and re-layouts  2.04 us (5%)
  other arithmetic  0.87 us (2%)
    ppermute x3, waiting for transfers between devices, from_behind(): return lax.ppermute(shard, axis, pairs)  23 us
    all_gather x1, blocking collectives, body(): gathered = lax.all_gather(latent, 'head', axis=0, tiled=True)  6.16 us
    ppermute x3, starting transfers between devices, from_behind(): return lax.ppermute(shard, axis, pairs)  5.73 us
    dot_general x4, matrix products, attend(): jnp.einsum('hqk,khd->hqd', rounded.astype(jnp.float32), key_value[:, :, N...  1.46 us
    dot_general x4, matrix products, attend(): jnp.einsum('qhd,khd->hqk', query_side, key_value[:, :, :NOPE], precision=...  1.25 us
    dot_general x4, matrix products, attend(): key_value = jnp.dot(key_latent, w_kv_up, preferred_element_type=jnp.float32)  0.97 us
    dot_general x4, matrix products, attend(): jnp.einsum('qhd,kd->hqk', query_rope, key_rope, preferred_element_type=jn...  0.94 us
  transfers between devices with their start and end apart: 3, of which 3 were waited for; matrix products, arithmetic and copies ran while one was open for 9% of the time, Pallas kernels for 0%

commit v1 on v0

--- a/solution.py
+++ b/solution.py
@@ -1,8 +1,11 @@
+import functools
 import math
 
 import jax
 import jax.numpy as jnp
 from jax import lax
+from jax.experimental import pallas as pl
+from jax.experimental.pallas import tpu as pltpu
 from jax.sharding import PartitionSpec as P
 
 D_LATENT = 256
@@ -111,7 +114,265 @@
     return finish(state, w_kv_up)
 
 
+LOG2E = 1.4426950408889634
+MESH = pl.DeviceIdType.MESH
+Z_UP, Y_SIDE, X_SIDE, CORE = range(4)
+
+
+def dot_rows(a, b):
+    return lax.dot_general(a, b, (((1,), (1,)), ((), ())), preferred_element_type=jnp.float32)
+
+
+def halves(x):
+    high = x.astype(jnp.bfloat16)
+    low = (x - high.astype(jnp.float32)).astype(jnp.bfloat16)
+    return high, low
+
+
+def relay_kernel(
+    planes, q_hbm, lat_hbm, w_hbm, out_ref,
+    keys, q_ref, w_ref, absorbed, rope, acc, row_max, row_sum,
+    load_sem, send_sem, recv_sem,
+):
+    seq, hd = lax.axis_index("seq"), lax.axis_index("head")
+    plane, side = seq // 2, seq % 2
+    core = hd % 2
+    chunk = lat_hbm.shape[0]
+    group = q_ref.shape[0]
+    heads = w_ref.shape[1] // (NOPE + VDIM)
+    other_side = seq + 1 - 2 * side
+    other_pair = (hd + 2) % 4
+    other_core = hd + 1 - 2 * core
+    targets = {
+        Z_UP: (seq + 2, hd),
+        Y_SIDE: (other_side, hd),
+        X_SIDE: (seq, other_pair),
+        CORE: (seq, other_core),
+    }
+
+    def copy(s, h, way):
+        index = s * 4 + h
+        rows = pl.ds(pl.multiple_of(index * chunk, chunk), chunk)
+        return pltpu.make_async_remote_copy(
+            src_ref=keys.at[rows],
+            dst_ref=keys.at[rows],
+            send_sem=send_sem.at[index, way],
+            recv_sem=recv_sem.at[index],
+            device_id=targets[way],
+            device_id_type=MESH,
+        )
+
+    own_rows = pl.ds(pl.multiple_of((seq * 4 + hd) * chunk, chunk), chunk)
+    load_own = pltpu.make_async_copy(lat_hbm, keys.at[own_rows], load_sem.at[0])
+    load_q = pltpu.make_async_copy(q_hbm, q_ref, load_sem.at[1])
+    load_w = pltpu.make_async_copy(w_hbm, w_ref, load_sem.at[2])
+    load_own.start()
+    load_q.start()
+    load_w.start()
+
+    barrier = pltpu.get_barrier_semaphore()
+    for way in (Y_SIDE, X_SIDE, CORE):
+        pl.semaphore_signal(barrier, inc=1, device_id=targets[way], device_id_type=MESH)
+
+    @pl.when(plane > 0)
+    def _():
+        pl.semaphore_signal(barrier, inc=1, device_id=(seq - 2, hd), device_id_type=MESH)
+
+    @pl.when(plane < planes - 1)
+    def _():
+        pl.semaphore_signal(barrier, inc=1, device_id=(seq + 2, hd), device_id_type=MESH)
+
+    has_below = jnp.where(plane > 0, 1, 0)
+    has_above = jnp.where(plane < planes - 1, 1, 0)
+    pl.semaphore_wait(barrier, 3 + has_below + has_above)
+
+    def here(k):
+        return (plane - k) * 2 + side
+
+    def across(k):
+        return (plane - k) * 2 + 1 - side
+
+    def column_sends(k):
+        s = here(k)
+        return [
+            (plane < planes - 1, s, hd, Z_UP),
+            (True if k else side == 0, s, hd, Y_SIDE),
+            (True, s, hd, X_SIDE),
+            (True, s, hd, CORE),
+        ]
+
+    def pair_sends(k):
+        s = here(k)
+        return [
+            ((core == 1) if k else (core == 1) & (side == 0), s, other_pair, Y_SIDE),
+            (True, s, other_pair, CORE),
+        ]
+
+    def side_sends(k):
+        s = across(k)
+        return [(core == 0, s, hd, X_SIDE), (True, s, hd, CORE)]
+
+    def corner_sends(k):
+        return [(True, across(k), other_pair, CORE)]
+
+    def guarded(condition, action):
+        if condition is True:
+            action()
+        else:
+            pl.when(condition)(action)
+
+    def start_all(sends):
+        for condition, s, h, way in sends:
+            guarded(condition, lambda s=s, h=h, way=way: copy(s, h, way).start())
+
+    def drain_all(sends):
+        for condition, s, h, way in sends:
+            guarded(condition, lambda s=s, h=h, way=way: copy(s, h, way).wait_send())
+
+    def arrived(s, h):
+        copy(s, h, CORE).wait_recv()
+
+    def when_plane(k, action):
+        guarded(True if k == 0 else plane >= k, action)
+
+    def when_across(k, action):
+        guarded(side == 1 if k == 0 else plane >= k, action)
+
+    load_own.wait()
+    start_all(column_sends(0))
+
+    load_q.wait()
+    load_w.wait()
+    for i in range(heads):
+        left = i * (NOPE + ROPE)
+        key_up = w_ref[:, i * (NOPE + VDIM):i * (NOPE + VDIM) + NOPE]
+        mixed = dot_rows(q_ref[:, left:left + NOPE], key_up)
+        high, low = halves(mixed)
+        absorbed[i * group:(i + 1) * group] = high
+        absorbed[(heads + i) * group:(heads + i + 1) * group] = low
+        rope[i * group:(i + 1) * group] = q_ref[:, left + NOPE:left + NOPE + ROPE]
+    row_max[...] = jnp.full_like(row_max, MASKED)
+    row_sum[...] = jnp.zeros_like(row_sum)
+    acc[...] = jnp.zeros_like(acc)
+
+    scale = LOG2E * (NOPE + ROPE) ** (-0.5)
+    rows = heads * group
+
+    def attend_keys(first_row, count, diagonal):
+        block = pl.ds(pl.multiple_of(first_row, count), count)
+        lat = keys[block, :D_LATENT]
+        both = dot_rows(absorbed[...], lat)
+        scores = both[:rows] + both[rows:] + dot_rows(rope[...], keys[block, D_LATENT:])
+        scores = scores * scale
+        if diagonal:
+            q_pos = lax.broadcasted_iota(jnp.int32, (rows, count), 0) % group
+            k_pos = lax.broadcasted_iota(jnp.int32, (rows, count), 1)
+            allowed = k_pos <= q_pos
+            scores = jnp.where(allowed, scores, MASKED)
+        old_max = row_max[...]
+        new_max = jnp.maximum(old_max, jnp.max(scores, axis=1, keepdims=True))
+        factor = jnp.exp2(old_max - new_max)
+        weights = jnp.exp2(scores - new_max[:, :1])
+        if diagonal:
+            weights = jnp.where(allowed, weights, 0.0)
+        row_max[...] = new_max
+        row_sum[...] = row_sum[...] * factor + jnp.sum(weights, axis=1, keepdims=True)
+        update = jnp.dot(weights.astype(jnp.bfloat16), lat, preferred_element_type=jnp.float32)
+        acc[...] = acc[...] * factor[:, :1] + update
+
+    def compute(k):
+        def own_group():
+            for h in (other_core, (other_core + 2) % 4):
+                arrived(here(k), h)
+            if k == 0:
+                attend_keys(seq * group, group, True)
+
+        def other_group():
+            for h in (other_core, (other_core + 2) % 4):
+                arrived(across(k), h)
+            if k == 0:
+                attend_keys((seq - 1) * group, group, False)
+            else:
+                attend_keys((plane - k) * 2 * group, 2 * group, False)
+
+        when_plane(k, own_group)
+        when_across(k, other_group)
+
+    for slot in range(1, planes + 3):
+        if slot < planes:
+            def column(k=slot):
+                arrived(here(k), hd)
+                start_all(column_sends(k))
+
+            when_plane(slot, column)
+        k = slot - 1
+        if 0 <= k < planes:
+            def pair_part(k=k):
+                arrived(here(k), other_pair)
+                start_all(pair_sends(k))
+
+            def side_part(k=k):
+                arrived(across(k), hd)
+                start_all(side_sends(k))
+
+            when_plane(k, pair_part)
+            when_across(k, side_part)
+        k = slot - 2
+        if 0 <= k < planes:
+            def corner_part(k=k):
+                arrived(across(k), other_pair)
+                start_all(corner_sends(k))
+
+            when_across(k, corner_part)
+        k = slot - 3
+        if 0 <= k < planes:
+            compute(k)
+
+    for i in range(heads):
+        value_up = w_ref[:, i * (NOPE + VDIM) + NOPE:(i + 1) * (NOPE + VDIM)]
+        part = slice(i * group, (i + 1) * group)
+        high, low = halves(acc[part])
+        result = jnp.dot(high, value_up, preferred_element_type=jnp.float32)
+        result = result + jnp.dot(low, value_up, preferred_element_type=jnp.float32)
+        out_ref[:, i * VDIM:(i + 1) * VDIM] = (result / row_sum[part, :VDIM]).astype(out_ref.dtype)
+
+    for k in range(planes):
+        when_plane(k, lambda k=k: drain_all(column_sends(k) + pair_sends(k)))
+        when_across(k, lambda k=k: drain_all(side_sends(k) + corner_sends(k)))
+
+
+def relay_body(queries, latent, w_kv_up):
+    seq_groups = lax.axis_size("seq")
+    group = queries.shape[0]
+    total = group * seq_groups
+    heads = w_kv_up.shape[1] // (NOPE + VDIM)
+    rows = heads * group
+    chunks = total // latent.shape[0]
+    return pl.pallas_call(
+        functools.partial(relay_kernel, seq_groups // 2),
+        out_shape=jax.ShapeDtypeStruct((group, heads * VDIM), jnp.bfloat16),
+        in_specs=[pl.BlockSpec(memory_space=pl.ANY)] * 3,
+        out_specs=pl.BlockSpec(memory_space=pltpu.VMEM),
+        scratch_shapes=[
+            pltpu.VMEM((total, latent.shape[1]), jnp.bfloat16),
+            pltpu.VMEM(queries.shape, jnp.bfloat16),
+            pltpu.VMEM(w_kv_up.shape, jnp.bfloat16),
+            pltpu.VMEM((2 * rows, D_LATENT), jnp.bfloat16),
+            pltpu.VMEM((rows, ROPE), jnp.bfloat16),
+            pltpu.VMEM((rows, D_LATENT), jnp.float32),
+            pltpu.VMEM((rows, 128), jnp.float32),
+            pltpu.VMEM((rows, 128), jnp.float32),
+            pltpu.SemaphoreType.DMA((3,)),
+            pltpu.SemaphoreType.DMA((chunks, 4)),
+            pltpu.SemaphoreType.DMA((chunks,)),
+        ],
+        compiler_params=pltpu.CompilerParams(collective_id=0, has_side_effects=True),
+    )(queries, latent, w_kv_up)
+
+
 def solution(mesh):
     in_specs = (P("seq", "head"), P(("seq", "head"), None), P(None, "head"))
     out_specs = P("seq", "head")
-    return jax.shard_map(body, mesh=mesh, in_specs=in_specs, out_specs=out_specs, check_vma=False)
+    small = mesh.shape["seq"] <= 16 and mesh.shape["seq"] % 2 == 0 and mesh.shape["head"] == 4
+    chosen = relay_body if small else body
+    return jax.shard_map(chosen, mesh=mesh, in_specs=in_specs, out_specs=out_specs, check_vma=False)

time: 42.9 us -> 21 us (0.49)
  waiting for transfers between devices: 23 us -> 0 us
  Pallas kernels: 0 us -> 19.3 us
  blocking collectives: 6.16 us -> 0 us
  starting transfers between devices: 5.73 us -> 0 us
  matrix products: 4.62 us -> 0 us
  other arithmetic: 0.87 us -> 0 us
  local copies, waits for them, and re-layouts: 2.04 us -> 1.47 us
    ppermute x3 -> x0, waiting for transfers between devices: 23 us -> none  [from_behind(): return lax.ppermute(shard, axis, pairs)]
    pallas_call x0 -> x1, Pallas kernels: none -> 19.3 us  [relay_body(): pl.pallas_call(functools.partial(relay_kernel, seq_groups // 2), out_shap...]
    all_gather x1 -> x0, blocking collectives: 6.16 us -> none  [body(): gathered = lax.all_gather(latent, 'head', axis=0, tiled=True)]
    ppermute x3 -> x0, starting transfers between devices: 5.73 us -> none  [from_behind(): return lax.ppermute(shard, axis, pairs)]
    dot_general x16 -> x0, matrix products: 4.62 us -> none  [the longest x4 1.46 us: attend(): jnp.einsum('hqk,khd->hqd', rounded.astype(jnp.float32), key_value[:, :, N...]
    unnamed x5 -> x1, local copies, waits for them, and re-layouts: 0.13 us -> 1.47 us
    convert_element_type x1 -> x0, local copies, waits for them, and re-layouts: 0.74 us -> none  [finish(): jnp.transpose(result, (1, 0, 2)).reshape(row_count, local_heads * VDIM)]
    reshape x3 -> x0, local copies, waits for them, and re-layouts: 0.68 us -> none  [attend(): key_value = key_value.reshape(key_count, local_heads, NOPE + VDIM)]
  transfers between devices with their start and end apart: 3 -> 0, of which waited for: 3 -> 0; matrix products, arithmetic and copies ran while one was open for 9% -> 0% of each run, Pallas kernels for 0% -> 0%
where the time goes in v1:
time: 21 us; the launch traced here: 20.8 us
  Pallas kernels  19.3 us (92%)
  local copies, waits for them, and re-layouts  1.47 us (7%)
    pallas_call x1, Pallas kernels, relay_body(): pl.pallas_call(functools.partial(relay_kernel, seq_groups // 2), out_shap...  19.3 us
    unnamed x1, local copies, waits for them, and re-layouts  1.47 us

profile of v1, /device:TPU:25, one launch (start us, length us, event | category | flops | bytes accessed | tf_op | source)
XLA Modules:
  0.0 20.8 jit_solution(504452042226478757)
XLA Ops:
  0.0 19.3 %shard_map.37 = bf16[128,256]{1,0:T(8,128)(2,1)} custom-call(bf16[128,384]{1,0:T(8,128)(2,1)} %q_hbm.1, bf16[32,320]{1,0:T(8,128)(2,1)} %lat_hbm.1, bf16[256,512]{1,0:T(8,128)(2,1)} %w_hbm.1), custom_call_target="tpu_custom_call" | custom-call | tf_op jit(solution)/shard_map/pallas_call | solution.py:351
  19.3 1.5 %copy.5 = bf16[128,256]{1,0:T(8,128)(2,1)} copy(bf16[128,256]{1,0:T(8,128)(2,1)} %shard_map.37) | data formatting | bytes 131072

commit v2 on v1

--- a/solution.py
+++ b/solution.py
@@ -116,9 +116,6 @@
 
 LOG2E = 1.4426950408889634
 MESH = pl.DeviceIdType.MESH
-Z_UP, Y_SIDE, X_SIDE, CORE = range(4)
-
-
 def dot_rows(a, b):
     return lax.dot_general(a, b, (((1,), (1,)), ((), ())), preferred_element_type=jnp.float32)
 
@@ -136,84 +133,53 @@
 ):
     seq, hd = lax.axis_index("seq"), lax.axis_index("head")
     plane, side = seq // 2, seq % 2
-    core = hd % 2
+    pair, core = hd // 2, hd % 2
     chunk = lat_hbm.shape[0]
     group = q_ref.shape[0]
     heads = w_ref.shape[1] // (NOPE + VDIM)
-    other_side = seq + 1 - 2 * side
-    other_pair = (hd + 2) % 4
-    other_core = hd + 1 - 2 * core
-    targets = {
-        Z_UP: (seq + 2, hd),
-        Y_SIDE: (other_side, hd),
-        X_SIDE: (seq, other_pair),
-        CORE: (seq, other_core),
-    }
-
-    def copy(s, h, way):
-        index = s * 4 + h
+    across = seq + 1 - 2 * side
+    other_pair = 1 - pair
+    other_core = 1 - core
+
+    def slot_of(s, p, c):
+        return (c * planes * 2 + s) * 2 + p
+
+    def copy(index, target_seq, target_head, way):
         rows = pl.ds(pl.multiple_of(index * chunk, chunk), chunk)
         return pltpu.make_async_remote_copy(
             src_ref=keys.at[rows],
             dst_ref=keys.at[rows],
             send_sem=send_sem.at[index, way],
             recv_sem=recv_sem.at[index],
-            device_id=targets[way],
+            device_id=(target_seq, target_head),
             device_id_type=MESH,
         )
 
-    own_rows = pl.ds(pl.multiple_of((seq * 4 + hd) * chunk, chunk), chunk)
+    own = slot_of(seq, pair, core)
+    own_rows = pl.ds(pl.multiple_of(own * chunk, chunk), chunk)
     load_own = pltpu.make_async_copy(lat_hbm, keys.at[own_rows], load_sem.at[0])
     load_q = pltpu.make_async_copy(q_hbm, q_ref, load_sem.at[1])
     load_w = pltpu.make_async_copy(w_hbm, w_ref, load_sem.at[2])
     load_own.start()
+
+    in_plane = [
+        (across, other_pair * 2 + core),
+        (across, hd),
+        (seq, other_pair * 2 + core),
+        (seq, pair * 2 + other_core),
+    ]
+    barrier = pltpu.get_barrier_semaphore()
+    for gap in range(planes - 1, 0, -1):
+        @pl.when(plane >= gap)
+        def _(gap=gap):
+            pl.semaphore_signal(
+                barrier, inc=1, device_id=(seq - 2 * gap, hd), device_id_type=MESH
+            )
+    for target in in_plane:
+        pl.semaphore_signal(barrier, inc=1, device_id=target, device_id_type=MESH)
     load_q.start()
     load_w.start()
-
-    barrier = pltpu.get_barrier_semaphore()
-    for way in (Y_SIDE, X_SIDE, CORE):
-        pl.semaphore_signal(barrier, inc=1, device_id=targets[way], device_id_type=MESH)
-
-    @pl.when(plane > 0)
-    def _():
-        pl.semaphore_signal(barrier, inc=1, device_id=(seq - 2, hd), device_id_type=MESH)
-
-    @pl.when(plane < planes - 1)
-    def _():
-        pl.semaphore_signal(barrier, inc=1, device_id=(seq + 2, hd), device_id_type=MESH)
-
-    has_below = jnp.where(plane > 0, 1, 0)
-    has_above = jnp.where(plane < planes - 1, 1, 0)
-    pl.semaphore_wait(barrier, 3 + has_below + has_above)
-
-    def here(k):
-        return (plane - k) * 2 + side
-
-    def across(k):
-        return (plane - k) * 2 + 1 - side
-
-    def column_sends(k):
-        s = here(k)
-        return [
-            (plane < planes - 1, s, hd, Z_UP),
-            (True if k else side == 0, s, hd, Y_SIDE),
-            (True, s, hd, X_SIDE),
-            (True, s, hd, CORE),
-        ]
-
-    def pair_sends(k):
-        s = here(k)
-        return [
-            ((core == 1) if k else (core == 1) & (side == 0), s, other_pair, Y_SIDE),
-            (True, s, other_pair, CORE),
-        ]
-
-    def side_sends(k):
-        s = across(k)
-        return [(core == 0, s, hd, X_SIDE), (True, s, hd, CORE)]
-
-    def corner_sends(k):
-        return [(True, across(k), other_pair, CORE)]
+    pl.semaphore_wait(barrier, len(in_plane) + planes - 1 - plane)
 
     def guarded(condition, action):
         if condition is True:
@@ -221,16 +187,40 @@
         else:
             pl.when(condition)(action)
 
+    def climb_sends():
+        return [
+            (plane + gap < planes, copy(own, seq + 2 * gap, hd, gap + 3))
+            for gap in range(planes - 1, 0, -1)
+        ]
+
+    def plane_sends(k):
+        index = slot_of(seq - 2 * k, pair, core)
+        to_across = True if k else side == 0
+        flags = (to_across, to_across, True, True)
+        return [
+            (flag, copy(index, target[0], target[1], way))
+            for way, (flag, target) in enumerate(zip(flags, in_plane))
+        ]
+
+    def core_send(index):
+        return (True, copy(index, in_plane[3][0], in_plane[3][1], 3))
+
+    def own_pair_sends(k):
+        return [core_send(slot_of(seq - 2 * k, other_pair, core))]
+
+    def across_sends(k):
+        return [core_send(slot_of(across - 2 * k, p, core)) for p in (pair, other_pair)]
+
     def start_all(sends):
-        for condition, s, h, way in sends:
-            guarded(condition, lambda s=s, h=h, way=way: copy(s, h, way).start())
+        for condition, item in sends:
+            guarded(condition, item.start)
 
     def drain_all(sends):
-        for condition, s, h, way in sends:
-            guarded(condition, lambda s=s, h=h, way=way: copy(s, h, way).wait_send())
-
-    def arrived(s, h):
-        copy(s, h, CORE).wait_recv()
+        for condition, item in sends:
+            guarded(condition, item.wait_send)
+
+    def arrived(index):
+        copy(index, in_plane[3][0], in_plane[3][1], 3).wait_recv()
 
     def when_plane(k, action):
         guarded(True if k == 0 else plane >= k, action)
@@ -239,7 +229,8 @@
         guarded(side == 1 if k == 0 else plane >= k, action)
 
     load_own.wait()
-    start_all(column_sends(0))
+    start_all(climb_sends())
+    start_all(plane_sends(0))
 
     load_q.wait()
     load_w.wait()
@@ -258,15 +249,18 @@
     scale = LOG2E * (NOPE + ROPE) ** (-0.5)
     rows = heads * group
 
-    def attend_keys(first_row, count, diagonal):
-        block = pl.ds(pl.multiple_of(first_row, count), count)
+    def attend_keys(first_slot, slots, key_core, diagonal):
+        count = slots * chunk
+        block = pl.ds(pl.multiple_of(first_slot * chunk, chunk), count)
         lat = keys[block, :D_LATENT]
         both = dot_rows(absorbed[...], lat)
         scores = both[:rows] + both[rows:] + dot_rows(rope[...], keys[block, D_LATENT:])
         scores = scores * scale
         if diagonal:
             q_pos = lax.broadcasted_iota(jnp.int32, (rows, count), 0) % group
-            k_pos = lax.broadcasted_iota(jnp.int32, (rows, count), 1)
+            q_pos = q_pos + (slots // 2 - 1) * group
+            k_row = lax.broadcasted_iota(jnp.int32, (rows, count), 1)
+            k_pos = (k_row // chunk * 2 + key_core) * chunk + k_row % chunk
             allowed = k_pos <= q_pos
             scores = jnp.where(allowed, scores, MASKED)
         old_max = row_max[...]
@@ -280,53 +274,60 @@
         update = jnp.dot(weights.astype(jnp.bfloat16), lat, preferred_element_type=jnp.float32)
         acc[...] = acc[...] * factor[:, :1] + update
 
-    def compute(k):
-        def own_group():
-            for h in (other_core, (other_core + 2) % 4):
-                arrived(here(k), h)
-            if k == 0:
-                attend_keys(seq * group, group, True)
-
-        def other_group():
-            for h in (other_core, (other_core + 2) % 4):
-                arrived(across(k), h)
-            if k == 0:
-                attend_keys((seq - 1) * group, group, False)
-            else:
-                attend_keys((plane - k) * 2 * group, 2 * group, False)
-
-        when_plane(k, own_group)
-        when_across(k, other_group)
-
-    for slot in range(1, planes + 3):
-        if slot < planes:
-            def column(k=slot):
-                arrived(here(k), hd)
-                start_all(column_sends(k))
-
-            when_plane(slot, column)
-        k = slot - 1
-        if 0 <= k < planes:
-            def pair_part(k=k):
-                arrived(here(k), other_pair)
-                start_all(pair_sends(k))
-
-            def side_part(k=k):
-                arrived(across(k), hd)
-                start_all(side_sends(k))
-
-            when_plane(k, pair_part)
-            when_across(k, side_part)
-        k = slot - 2
-        if 0 <= k < planes:
-            def corner_part(k=k):
-                arrived(across(k), other_pair)
-                start_all(corner_sends(k))
-
-            when_across(k, corner_part)
-        k = slot - 3
-        if 0 <= k < planes:
-            compute(k)
+    def compute(k, key_core):
+        first = slot_of((plane - k) * 2, 0, key_core)
+        if k == 0:
+            pl.when(side == 0)(lambda: attend_keys(first, 2, key_core, True))
+            pl.when(side == 1)(lambda: attend_keys(first, 4, key_core, True))
+        else:
+            pl.when(plane >= k)(lambda: attend_keys(first, 4, key_core, False))
+
+    def from_below(k):
+        def action():
+            arrived(slot_of(seq - 2 * k, pair, core))
+            start_all(plane_sends(k))
+
+        when_plane(k, action)
+
+    def from_plane(k):
+        def own_side():
+            arrived(slot_of(seq - 2 * k, other_pair, core))
+            start_all(own_pair_sends(k))
+
+        def other_side():
+            for p in (pair, other_pair):
+                arrived(slot_of(across - 2 * k, p, core))
+            start_all(across_sends(k))
+
+        when_plane(k, own_side)
+        when_across(k, other_side)
+
+    def from_core(k):
+        def own_side():
+            for p in (pair, other_pair):
+                arrived(slot_of(seq - 2 * k, p, other_core))
+
+        def other_side():
+            for p in (pair, other_pair):
+                arrived(slot_of(across - 2 * k, p, other_core))
+
+        when_plane(k, own_side)
+        when_across(k, other_side)
+
+    for k in range(1, planes):
+        if k == 2:
+            from_plane(0)
+        from_below(k)
+    if planes < 3:
+        from_plane(0)
+    compute(0, core)
+    for k in range(1, planes):
+        from_plane(k)
+        from_core(k - 1)
+        compute(k - 1, other_core)
+        compute(k, core)
+    from_core(planes - 1)
+    compute(planes - 1, other_core)
 
     for i in range(heads):
         value_up = w_ref[:, i * (NOPE + VDIM) + NOPE:(i + 1) * (NOPE + VDIM)]
@@ -336,9 +337,10 @@
         result = result + jnp.dot(low, value_up, preferred_element_type=jnp.float32)
         out_ref[:, i * VDIM:(i + 1) * VDIM] = (result / row_sum[part, :VDIM]).astype(out_ref.dtype)
 
+    drain_all(climb_sends())
     for k in range(planes):
-        when_plane(k, lambda k=k: drain_all(column_sends(k) + pair_sends(k)))
-        when_across(k, lambda k=k: drain_all(side_sends(k) + corner_sends(k)))
+        when_plane(k, lambda k=k: drain_all(plane_sends(k) + own_pair_sends(k)))
+        when_across(k, lambda k=k: drain_all(across_sends(k)))
 
 
 def relay_body(queries, latent, w_kv_up):
@@ -350,8 +352,8 @@
     chunks = total // latent.shape[0]
     return pl.pallas_call(
         functools.partial(relay_kernel, seq_groups // 2),
-        out_shape=jax.ShapeDtypeStruct((group, heads * VDIM), jnp.bfloat16),
-        in_specs=[pl.BlockSpec(memory_space=pl.ANY)] * 3,
+        out_shape=pltpu.VMEM((group, heads * VDIM), jnp.bfloat16),
+        in_specs=[pl.BlockSpec(memory_space=pltpu.HBM)] * 3,
         out_specs=pl.BlockSpec(memory_space=pltpu.VMEM),
         scratch_shapes=[
             pltpu.VMEM((total, latent.shape[1]), jnp.bfloat16),
@@ -363,7 +365,7 @@
             pltpu.VMEM((rows, 128), jnp.float32),
             pltpu.VMEM((rows, 128), jnp.float32),
             pltpu.SemaphoreType.DMA((3,)),
-            pltpu.SemaphoreType.DMA((chunks, 4)),
+            pltpu.SemaphoreType.DMA((chunks, seq_groups // 2 + 3)),
             pltpu.SemaphoreType.DMA((chunks,)),
         ],
         compiler_params=pltpu.CompilerParams(collective_id=0, has_side_effects=True),

time: 21 us -> 16.3 us (0.78)
  Pallas kernels: 19.3 us -> 15.5 us
  local copies, waits for them, and re-layouts: 1.47 us -> 0.63 us
    pallas_call x1, Pallas kernels: 19.3 us -> 15.5 us  [relay_body(): pl.pallas_call(functools.partial(relay_kernel, seq_groups // 2), out_shap...]
    unnamed x1, local copies, waits for them, and re-layouts: 1.47 us -> 0.63 us
where the time goes in v2:
time: 16.3 us; the launch traced here: 16.2 us
  Pallas kernels  15.5 us (95%)
  local copies, waits for them, and re-layouts  0.63 us (4%)
    pallas_call x1, Pallas kernels, relay_body(): pl.pallas_call(functools.partial(relay_kernel, seq_groups // 2), out_shap...  15.5 us
    unnamed x1, local copies, waits for them, and re-layouts  0.63 us

profile of v2, /device:TPU:25, one launch (start us, length us, event | category | flops | bytes accessed | tf_op | source)
XLA Modules:
  0.0 16.2 jit_solution(8799965735775101887)
XLA Ops:
  0.0 15.5 %shard_map.37 = bf16[128,256]{1,0:T(8,128)(2,1)S(1)} custom-call(bf16[128,384]{1,0:T(8,128)(2,1)} %q_hbm.1, bf16[32,320]{1,0:T(8,128)(2,1)} %lat_hbm.1, bf16[256,512]{1,0:T(8,128)(2,1)} %w_hbm.1), custom_call_target="tpu_custom_call" | custom-call | tf_op jit(solution)/shard_map/pallas_call | solution.py:353
  15.5 0.6 %copy.5 = bf16[128,256]{1,0:T(8,128)(2,1)} copy(bf16[128,256]{1,0:T(8,128)(2,1)S(1)} %shard_map.37) | data formatting | bytes 131072

commit v3 on v2

--- a/solution.py
+++ b/solution.py
@@ -129,7 +129,7 @@
 def relay_kernel(
     planes, q_hbm, lat_hbm, w_hbm, out_ref,
     keys, q_ref, w_ref, absorbed, rope, acc, row_max, row_sum,
-    load_sem, send_sem, recv_sem,
+    load_sem, climb_sem, send_sem, recv_sem, ready_sem,
 ):
     seq, hd = lax.axis_index("seq"), lax.axis_index("head")
     plane, side = seq // 2, seq % 2
@@ -144,14 +144,16 @@
     def slot_of(s, p, c):
         return (c * planes * 2 + s) * 2 + p
 
-    def copy(index, target_seq, target_head, way):
-        rows = pl.ds(pl.multiple_of(index * chunk, chunk), chunk)
+    def region(index, count):
+        return keys.at[pl.ds(pl.multiple_of(index * chunk, chunk), count * chunk)]
+
+    def copy(index, target, sent, landed, count=1):
         return pltpu.make_async_remote_copy(
-            src_ref=keys.at[rows],
-            dst_ref=keys.at[rows],
-            send_sem=send_sem.at[index, way],
-            recv_sem=recv_sem.at[index],
-            device_id=(target_seq, target_head),
+            src_ref=region(index, count),
+            dst_ref=region(index, count),
+            send_sem=sent,
+            recv_sem=landed,
+            device_id=target,
             device_id_type=MESH,
         )
 
@@ -162,24 +164,36 @@
     load_w = pltpu.make_async_copy(w_hbm, w_ref, load_sem.at[2])
     load_own.start()
 
-    in_plane = [
-        (across, other_pair * 2 + core),
-        (across, hd),
-        (seq, other_pair * 2 + core),
-        (seq, pair * 2 + other_core),
-    ]
+    across_peer = (across, hd)
+    pair_peer = (seq, other_pair * 2 + core)
+    corner_peer = (across, other_pair * 2 + core)
+    core_peer = (seq, pair * 2 + other_core)
+    below, above = (seq - 2, hd), (seq + 2, hd)
+    has_below, has_above = plane > 0, plane < planes - 1
+
     barrier = pltpu.get_barrier_semaphore()
-    for gap in range(planes - 1, 0, -1):
-        @pl.when(plane >= gap)
-        def _(gap=gap):
-            pl.semaphore_signal(
-                barrier, inc=1, device_id=(seq - 2 * gap, hd), device_id_type=MESH
-            )
-    for target in in_plane:
+
+    @pl.when(has_below)
+    def _():
+        pl.semaphore_signal(barrier, inc=1, device_id=below, device_id_type=MESH)
+
+    for target in (pair_peer, across_peer, core_peer):
         pl.semaphore_signal(barrier, inc=1, device_id=target, device_id_type=MESH)
+
+    @pl.when(has_above)
+    def _():
+        pl.semaphore_signal(barrier, inc=1, device_id=above, device_id_type=MESH)
+
     load_q.start()
     load_w.start()
-    pl.semaphore_wait(barrier, len(in_plane) + planes - 1 - plane)
+    pl.semaphore_wait(barrier, 3 + jnp.where(has_below, 1, 0) + jnp.where(has_above, 1, 0))
+
+    def pass_down(gap):
+        pl.semaphore_signal(ready_sem.at[gap], inc=1, device_id=below, device_id_type=MESH)
+
+    if planes > 2:
+        pl.when(has_below & has_above)(lambda: pass_down(2))
+    pl.semaphore_signal(ready_sem.at[0], inc=1, device_id=pair_peer, device_id_type=MESH)
 
     def guarded(condition, action):
         if condition is True:
@@ -187,40 +201,26 @@
         else:
             pl.when(condition)(action)
 
-    def climb_sends():
-        return [
-            (plane + gap < planes, copy(own, seq + 2 * gap, hd, gap + 3))
-            for gap in range(planes - 1, 0, -1)
-        ]
-
-    def plane_sends(k):
+    BELOW, PAIR, ACROSS, CORNER, CORE = range(5)
+
+    def climb(gap):
+        return copy(own, (seq + 2 * gap, hd), climb_sem.at[gap], recv_sem.at[gap, BELOW])
+
+    def send(index, k, target, kind):
+        copy(index, target, send_sem.at[k], recv_sem.at[k, kind]).start()
+
+    def send_sides(k):
         index = slot_of(seq - 2 * k, pair, core)
-        to_across = True if k else side == 0
-        flags = (to_across, to_across, True, True)
-        return [
-            (flag, copy(index, target[0], target[1], way))
-            for way, (flag, target) in enumerate(zip(flags, in_plane))
-        ]
-
-    def core_send(index):
-        return (True, copy(index, in_plane[3][0], in_plane[3][1], 3))
-
-    def own_pair_sends(k):
-        return [core_send(slot_of(seq - 2 * k, other_pair, core))]
-
-    def across_sends(k):
-        return [core_send(slot_of(across - 2 * k, p, core)) for p in (pair, other_pair)]
-
-    def start_all(sends):
-        for condition, item in sends:
-            guarded(condition, item.start)
-
-    def drain_all(sends):
-        for condition, item in sends:
-            guarded(condition, item.wait_send)
-
-    def arrived(index):
-        copy(index, in_plane[3][0], in_plane[3][1], 3).wait_recv()
+        guarded(True if k else side == 0, lambda: send(index, k, across_peer, ACROSS))
+        send(index, k, pair_peer, PAIR)
+        send(index, k, core_peer, CORE)
+
+    def send_corner(k):
+        index = slot_of(seq - 2 * k, pair, core)
+        guarded(True if k else side == 0, lambda: send(index, k, corner_peer, CORNER))
+
+    def arrived(index, k, kind, count=1):
+        copy(index, core_peer, send_sem.at[k], recv_sem.at[k, kind], count).wait_recv()
 
     def when_plane(k, action):
         guarded(True if k == 0 else plane >= k, action)
@@ -229,8 +229,18 @@
         guarded(side == 1 if k == 0 else plane >= k, action)
 
     load_own.wait()
-    start_all(climb_sends())
-    start_all(plane_sends(0))
+    if planes > 1:
+        pl.when(has_above)(lambda: climb(1).start())
+    send_sides(0)
+    pl.semaphore_wait(ready_sem.at[0], 1)
+    send_corner(0)
+    for gap in range(2, planes):
+        @pl.when(plane + gap < planes)
+        def _(gap=gap):
+            pl.semaphore_wait(ready_sem.at[gap], 1)
+            if gap + 1 < planes:
+                pl.when(has_below)(lambda: pass_down(gap + 1))
+            climb(gap).start()
 
     load_q.wait()
     load_w.wait()
@@ -284,47 +294,49 @@
 
     def from_below(k):
         def action():
-            arrived(slot_of(seq - 2 * k, pair, core))
-            start_all(plane_sends(k))
+            arrived(slot_of(seq - 2 * k, pair, core), k, BELOW)
+            send_corner(k)
+            send_sides(k)
 
         when_plane(k, action)
 
     def from_plane(k):
         def own_side():
-            arrived(slot_of(seq - 2 * k, other_pair, core))
-            start_all(own_pair_sends(k))
+            index = slot_of(seq - 2 * k, other_pair, core)
+            arrived(index, k, PAIR)
+            send(index, k, core_peer, CORE)
 
         def other_side():
-            for p in (pair, other_pair):
-                arrived(slot_of(across - 2 * k, p, core))
-            start_all(across_sends(k))
+            for p, kind in ((pair, ACROSS), (other_pair, CORNER)):
+                index = slot_of(across - 2 * k, p, core)
+                arrived(index, k, kind)
+                send(index, k, core_peer, CORE)
 
         when_plane(k, own_side)
         when_across(k, other_side)
 
     def from_core(k):
-        def own_side():
-            for p in (pair, other_pair):
-                arrived(slot_of(seq - 2 * k, p, other_core))
-
-        def other_side():
-            for p in (pair, other_pair):
-                arrived(slot_of(across - 2 * k, p, other_core))
-
-        when_plane(k, own_side)
-        when_across(k, other_side)
-
+        first = slot_of((plane - k) * 2, 0, other_core)
+        if k == 0:
+            pl.when(side == 0)(lambda: arrived(first, k, CORE, 2))
+            pl.when(side == 1)(lambda: arrived(first, k, CORE, 4))
+        else:
+            pl.when(plane >= k)(lambda: arrived(first, k, CORE, 4))
+
+    for k in range(planes):
+        if k > 0:
+            from_below(k)
+        if k == 1 or planes == 1:
+            from_plane(0)
+        if k == 2 or planes <= 2 and k == planes - 1:
+            compute(0, core)
+            if planes > 1:
+                from_plane(1)
     for k in range(1, planes):
-        if k == 2:
-            from_plane(0)
-        from_below(k)
-    if planes < 3:
-        from_plane(0)
-    compute(0, core)
-    for k in range(1, planes):
-        from_plane(k)
         from_core(k - 1)
         compute(k - 1, other_core)
+        if k + 1 < planes:
+            from_plane(k + 1)
         compute(k, core)
     from_core(planes - 1)
     compute(planes - 1, other_core)
@@ -337,10 +349,12 @@
         result = result + jnp.dot(low, value_up, preferred_element_type=jnp.float32)
         out_ref[:, i * VDIM:(i + 1) * VDIM] = (result / row_sum[part, :VDIM]).astype(out_ref.dtype)
 
-    drain_all(climb_sends())
+    for gap in range(1, planes):
+        pl.when(plane + gap < planes)(lambda gap=gap: climb(gap).wait_send())
     for k in range(planes):
-        when_plane(k, lambda k=k: drain_all(plane_sends(k) + own_pair_sends(k)))
-        when_across(k, lambda k=k: drain_all(across_sends(k)))
+        copies = 7 if k else 5
+        sent = copy(0, core_peer, send_sem.at[k], recv_sem.at[k, CORE], copies)
+        when_plane(k, sent.wait_send)
 
 
 def relay_body(queries, latent, w_kv_up):
@@ -349,9 +363,9 @@
     total = group * seq_groups
     heads = w_kv_up.shape[1] // (NOPE + VDIM)
     rows = heads * group
-    chunks = total // latent.shape[0]
+    planes = seq_groups // 2
     return pl.pallas_call(
-        functools.partial(relay_kernel, seq_groups // 2),
+        functools.partial(relay_kernel, planes),
         out_shape=pltpu.VMEM((group, heads * VDIM), jnp.bfloat16),
         in_specs=[pl.BlockSpec(memory_space=pltpu.HBM)] * 3,
         out_specs=pl.BlockSpec(memory_space=pltpu.VMEM),
@@ -365,8 +379,10 @@
             pltpu.VMEM((rows, 128), jnp.float32),
             pltpu.VMEM((rows, 128), jnp.float32),
             pltpu.SemaphoreType.DMA((3,)),
-            pltpu.SemaphoreType.DMA((chunks, seq_groups // 2 + 3)),
-            pltpu.SemaphoreType.DMA((chunks,)),
+            pltpu.SemaphoreType.DMA((planes,)),
+            pltpu.SemaphoreType.DMA((planes,)),
+            pltpu.SemaphoreType.DMA((planes, 5)),
+            pltpu.SemaphoreType.REGULAR((planes,)),
         ],
         compiler_params=pltpu.CompilerParams(collective_id=0, has_side_effects=True),
     )(queries, latent, w_kv_up)

time: 16.3 us -> 15 us (0.920)
  the two profiles are of different devices: /device:TPU:25 before, /device:TPU:24 now
where the time goes in v3:
time: 15 us; the launch traced here: 14.8 us
  Pallas kernels  14.2 us (95%)
  local copies, waits for them, and re-layouts  0.63 us (4%)
    pallas_call x1, Pallas kernels, relay_body(): pl.pallas_call(functools.partial(relay_kernel, planes), out_shape=pltpu.V...  14.2 us
    unnamed x1, local copies, waits for them, and re-layouts  0.63 us

profile of v3, /device:TPU:24, one launch (start us, length us, event | category | flops | bytes accessed | tf_op | source)
XLA Modules:
  0.0 14.8 jit_solution(8463730337326609034)
XLA Ops:
  0.0 14.2 %shard_map.37 = bf16[128,256]{1,0:T(8,128)(2,1)S(1)} custom-call(bf16[128,384]{1,0:T(8,128)(2,1)} %q_hbm.1, bf16[32,320]{1,0:T(8,128)(2,1)} %lat_hbm.1, bf16[256,512]{1,0:T(8,128)(2,1)} %w_hbm.1), custom_call_target="tpu_custom_call" | custom-call | tf_op jit(solution)/shard_map/pallas_call | solution.py:367
  14.2 0.6 %copy.5 = bf16[128,256]{1,0:T(8,128)(2,1)} copy(bf16[128,256]{1,0:T(8,128)(2,1)S(1)} %shard_map.37) | data formatting | bytes 131072

commit v4 on v3

--- a/solution.py
+++ b/solution.py
@@ -126,6 +126,11 @@
     return high, low
 
 
+def across_lanes(column, width):
+    repeats = -(-width // column.shape[1])
+    return jnp.concatenate([column] * repeats, axis=1)[:, :width]
+
+
 def relay_kernel(
     planes, q_hbm, lat_hbm, w_hbm, out_ref,
     keys, q_ref, w_ref, absorbed, rope, acc, row_max, row_sum,
@@ -276,13 +281,13 @@
         old_max = row_max[...]
         new_max = jnp.maximum(old_max, jnp.max(scores, axis=1, keepdims=True))
         factor = jnp.exp2(old_max - new_max)
-        weights = jnp.exp2(scores - new_max[:, :1])
+        weights = jnp.exp2(scores - across_lanes(new_max, count))
         if diagonal:
             weights = jnp.where(allowed, weights, 0.0)
         row_max[...] = new_max
         row_sum[...] = row_sum[...] * factor + jnp.sum(weights, axis=1, keepdims=True)
         update = jnp.dot(weights.astype(jnp.bfloat16), lat, preferred_element_type=jnp.float32)
-        acc[...] = acc[...] * factor[:, :1] + update
+        acc[...] = acc[...] * across_lanes(factor, D_LATENT) + update
 
     def compute(k, key_core):
         first = slot_of((plane - k) * 2, 0, key_core)
@@ -326,20 +331,19 @@
     for k in range(planes):
         if k > 0:
             from_below(k)
-        if k == 1 or planes == 1:
-            from_plane(0)
-        if k == 2 or planes <= 2 and k == planes - 1:
-            compute(0, core)
-            if planes > 1:
-                from_plane(1)
-    for k in range(1, planes):
-        from_core(k - 1)
-        compute(k - 1, other_core)
+        if 1 <= k <= 2:
+            from_plane(k - 1)
+    for k in range(min(planes - 1, 2), min(planes, 2)):
+        from_plane(k)
+    compute(0, core)
+    for k in range(planes):
+        from_core(k)
+        compute(k, other_core)
+        ahead = k + 2
+        if ahead < planes:
+            from_plane(ahead)
         if k + 1 < planes:
-            from_plane(k + 1)
-        compute(k, core)
-    from_core(planes - 1)
-    compute(planes - 1, other_core)
+            compute(k + 1, core)
 
     for i in range(heads):
         value_up = w_ref[:, i * (NOPE + VDIM) + NOPE:(i + 1) * (NOPE + VDIM)]

time: 15 us -> 14.5 us (0.967)
  the two profiles are of different devices: /device:TPU:24 before, /device:TPU:25 now
where the time goes in v4:
time: 14.5 us; the launch traced here: 14.2 us
  Pallas kernels  13.6 us (94%)
  local copies, waits for them, and re-layouts  0.63 us (4%)
    pallas_call x1, Pallas kernels, relay_body(): pl.pallas_call(functools.partial(relay_kernel, planes), out_shape=pltpu.V...  13.6 us
    unnamed x1, local copies, waits for them, and re-layouts  0.63 us

profile of v4, /device:TPU:25, one launch (start us, length us, event | category | flops | bytes accessed | tf_op | source)
XLA Modules:
  0.0 14.2 jit_solution(17364752625848199126)
XLA Ops:
  0.0 13.6 %shard_map.37 = bf16[128,256]{1,0:T(8,128)(2,1)S(1)} custom-call(bf16[128,384]{1,0:T(8,128)(2,1)} %q_hbm.1, bf16[32,320]{1,0:T(8,128)(2,1)} %lat_hbm.1, bf16[256,512]{1,0:T(8,128)(2,1)} %w_hbm.1), custom_call_target="tpu_custom_call" | custom-call | tf_op jit(solution)/shard_map/pallas_call | solution.py:371
  13.6 0.6 %copy.5 = bf16[128,256]{1,0:T(8,128)(2,1)} copy(bf16[128,256]{1,0:T(8,128)(2,1)S(1)} %shard_map.37) | data formatting | bytes 131072

commit v5 on v4

--- a/solution.py
+++ b/solution.py
@@ -328,22 +328,28 @@
         else:
             pl.when(plane >= k)(lambda: arrived(first, k, CORE, 4))
 
+    def attend_first():
+        compute(0, core)
+        from_core(0)
+        compute(0, other_core)
+
     for k in range(planes):
         if k > 0:
             from_below(k)
         if 1 <= k <= 2:
+            if k == 2:
+                attend_first()
             from_plane(k - 1)
-    for k in range(min(planes - 1, 2), min(planes, 2)):
-        from_plane(k)
-    compute(0, core)
-    for k in range(planes):
+    if planes < 3:
+        for k in range(planes - 1, planes):
+            from_plane(k)
+        attend_first()
+    for k in range(1, planes):
+        compute(k, core)
+        if k + 1 < planes and k + 1 >= 2:
+            from_plane(k + 1)
         from_core(k)
         compute(k, other_core)
-        ahead = k + 2
-        if ahead < planes:
-            from_plane(ahead)
-        if k + 1 < planes:
-            compute(k + 1, core)
 
     for i in range(heads):
         value_up = w_ref[:, i * (NOPE + VDIM) + NOPE:(i + 1) * (NOPE + VDIM)]

time: 14.5 us -> 14.3 us (0.986)
  no operation moved by 1% of the time
where the time goes in v5:
time: 14.3 us; the launch traced here: 14.1 us
  Pallas kernels  13.5 us (94%)
  local copies, waits for them, and re-layouts  0.63 us (4%)
    pallas_call x1, Pallas kernels, relay_body(): pl.pallas_call(functools.partial(relay_kernel, planes), out_shape=pltpu.V...  13.5 us
    unnamed x1, local copies, waits for them, and re-layouts  0.63 us

profile of v5, /device:TPU:25, one launch (start us, length us, event | category | flops | bytes accessed | tf_op | source)
XLA Modules:
  0.0 14.1 jit_solution(18168890289953989831)
XLA Ops:
  0.0 13.5 %shard_map.37 = bf16[128,256]{1,0:T(8,128)(2,1)S(1)} custom-call(bf16[128,384]{1,0:T(8,128)(2,1)} %q_hbm.1, bf16[32,320]{1,0:T(8,128)(2,1)} %lat_hbm.1, bf16[256,512]{1,0:T(8,128)(2,1)} %w_hbm.1), custom_call_target="tpu_custom_call" | custom-call | tf_op jit(solution)/shard_map/pallas_call | solution.py:377
  13.5 0.6 %copy.5 = bf16[128,256]{1,0:T(8,128)(2,1)} copy(bf16[128,256]{1,0:T(8,128)(2,1)S(1)} %shard_map.37) | data formatting | bytes 131072
